TPU v7x, 128 devices: a whole 4x4x4 slice. The times are simulated.
128 devices in a mesh: row: 32 (over z, x, core), col: 4 (over y).
Axes of the slice: x: 4, y: 4, z: 4, core: 2. Of those that a mesh axis runs over, the one named last changes fastest.
Arguments:
- prior_scores: float32 [12288, 12288], P('row', 'col'), may hold values from 0.001 to 10
- tiles_first: bfloat16 [96, 5, 128, 128], P('row'), may hold values from 0 to 1, as said below
- columns_first: int32 [96, 5], P('row'), may hold values from 0 to 95, as said below
- tiles_second: bfloat16 [96, 5, 128, 128], P('col'), may hold values from 0 to 1, as said below
- columns_second: int32 [96, 5], P('col'), may hold values from 0 to 95, as said below
Outputs:
- alignment: float32 [12288, 12288], P('row', 'col')
Inputs may be any that keep to these rules, and one draw needn't show every extreme that they name: `tiles_first`: in every block row, the block in the first slot has entries of 0.5 or more on its diagonal. `tiles_second`: in every block row, the block in the first slot has entries of 0.5 or more on its diagonal. `columns_first`: each block row lists 5 different block columns. `columns_second`: each block row lists 5 different block columns.
All inputs are finite; a program needn't handle non-finite values.
Results may differ from a plain program's by a relative error of at most 0.0004.
The roundings to bfloat16 on the way count: a program that leaves them out, or rounds other values in their place, can miss the bound.
Values may be sent and summed in bfloat16 or wider, within the bound.
A program may use at most 192 MiB of HBM per device.

v0:
```python
import functools
import jax
import jax.numpy as jnp
from jax import lax
from jax.sharding import Mesh
from jax.sharding import PartitionSpec as P

ITERS = 2
ROW = ("row_0", "row_1", "row_2")
ROW_COL = ("row_0", "row_1", "row_2", "col")
mixing = 0.8


def by_axis(value, axes):
    return functools.reduce(lax.psum, axes, value)


def second_product(features, tile_set, columns, inverse):
    tile_size = tile_set.shape[2]
    blocks = features.reshape(-1, tile_size, features.shape[1])
    picked = jnp.take(blocks, columns, axis=0)
    result = jnp.einsum("jsoi,jsin->jon", tile_set, picked, preferred_element_type=jnp.float32)
    result = result.reshape(-1, features.shape[1]) * inverse[:, None]
    return result.astype(jnp.bfloat16)


def first_product(slab_data, tile_set, columns, inverse):
    tile_size = tile_set.shape[2]
    blocks = slab_data.reshape(slab_data.shape[0], -1, tile_size)
    picked = jnp.take(blocks, columns, axis=1)
    result = jnp.einsum("cisk,isok->cio", picked, tile_set, preferred_element_type=jnp.float32)
    result = result.reshape(slab_data.shape[0], -1) * inverse[None, :]
    return result.astype(jnp.bfloat16)


def local(prior_scores, tiles_first, columns_first, tiles_second, columns_second):
    prior_cols = prior_scores.T
    row_count = lax.axis_size(ROW)
    cell_count = float(
        prior_scores.shape[0] * row_count * prior_scores.shape[1] * lax.axis_size("col")
    )
    all_first, all_columns = (
        lax.all_gather(tiles_first, ROW, axis=0, tiled=True),
        lax.all_gather(columns_first, ROW, axis=0, tiled=True),
    )
    inverse_first = 1.0 / jnp.sum(all_first, axis=(1, 3), dtype=jnp.float32).reshape(-1)
    inverse_second = 1.0 / jnp.sum(tiles_second, axis=(1, 3), dtype=jnp.float32).reshape(-1)
    prior_sum = by_axis(jnp.sum(prior_cols), ROW_COL)
    current_state = prior_cols
    for iteration in range(ITERS):
        current = current_state.astype(jnp.bfloat16)
        gathered = lax.all_gather(current, "col", axis=0, tiled=True)
        mixed_cols = second_product(gathered, tiles_second, columns_second, inverse_second)
        slab_data = lax.all_to_all(mixed_cols, ROW, split_axis=0, concat_axis=1, tiled=True)
        propagated = first_product(slab_data, all_first, all_columns, inverse_first)
        partial_value = jnp.sum(propagated.astype(jnp.float32))
        returned = lax.all_to_all(propagated, ROW, split_axis=1, concat_axis=0, tiled=True)
        slab_sum = by_axis(partial_value, ROW_COL)
        grand_total = mixing * slab_sum + (1.0 - mixing) * prior_sum
        updated = mixing * returned.astype(jnp.float32) + (1.0 - mixing) * prior_cols
        current_state = updated / (grand_total / cell_count)
    return current_state.T


def solution(mesh):
    finer = Mesh(
        mesh.devices.reshape(4, 4, 2, mesh.shape["col"]), ("row_0", "row_1", "row_2", "col")
    )
    return jax.shard_map(
        local,
        mesh=finer,
        in_specs=(
            P(ROW, "col"),
            P(ROW, None, None, None),
            P(ROW, None),
            P("col", None, None, None),
            P("col", None),
        ),
        out_specs=P(ROW, "col"),
        check_vma=False,
    )
```

profile of v0, /device:TPU:0, one launch (start us, length us, event | category | flops | bytes accessed | tf_op | source)
XLA Modules:
  0.0 633.5 jit_solution(3991835615490677281)
XLA Ops:
  6.5 7.0 %fusion.31 = (f32[]{:T(128)}, bf16[3072,384]{0,1:T(8,128)(2,1)}) fusion(f32[384,3072]{1,0:T(8,128)} %param.9), kind=kLoop, calls=%fused_computation.54 | loop fusion | flops 2359295 | bytes 7077892 | tf_op jit(solution)/shard_map/reduce_sum | solution.py:48
  17.4 90.7 %all-gather.5.cloned.1.call-done = bf16[12288,384]{0,1:T(8,128)(2,1)} async-done(((bf16[3072,384]{0,1:T(8,128)(2,1)}), bf16[12288,384]{0,1:T(8,128)(2,1)}) %all-gather.5.cloned.1.call-update) | async-done | bytes 9437200 | tf_op jit(solution)/shard_map/all_gather | solution.py:52
  108.1 12.6 %copy.59 = bf16[12288,384]{1,0:T(8,128)(2,1)} copy(bf16[12288,384]{0,1:T(8,128)(2,1)} %all-gather.5.cloned.1.call-done) | data formatting | bytes 18874368 | tf_op jit(solution)/shard_map/all_gather | solution.py:52
  120.7 12.7 %gather_fusion = bf16[120,128,384]{2,1,0:T(8,128)(2,1)} fusion(bf16[96,128,384]{2,1,0:T(8,128)(2,1)} %bitcast.69, s32[1024]{0:T(1024)S(1)} %pad_clamp_fusion.1), kind=kCustom, calls=%fused_computation.clone | custom fusion | bytes 23593440 | tf_op jit(solution)/shard_map/jit(_take)/gather | solution.py:21
  133.4 8.3 %fusion.8 = f32[24,384,128,1]{1,2,3,0:T(8,128)S(1)} fusion(bf16[24,5,128,128]{3,2,1,0:T(8,128)(2,1)} %param.12, bf16[24,5,128,384]{3,2,1,0:T(8,128)(2,1)} %bitcast.75, pred[24,5]{1,0:T(8,128)(4,1)S(1)} %copy.56), kind=kOutput, calls=%fused_computation.13 | convolution fusion | flops 1515847680 | bytes 20447352 | tf_op jit(solution)/shard_map/jsoi,jsin->jon/dot_general | solution.py:22
  143.6 7.2 %all-to-all-start = ((bf16[32,96,384]{2,1,0:T(8,128)(2,1)}), bf16[32,96,384]{2,1,0:T(8,128)(2,1)S(1)}, u32[]{:S(2)}, u32[]{:S(2)}) async-start(bf16[32,96,384]{2,1,0:T(8,128)(2,1)} %multiply_convert_fusion.5), calls=%async_computation | async-start | bytes 4718592 | tf_op jit(solution)/shard_map/all_to_all | solution.py:54
  150.9 70.6 %all-gather = s32[32,3,5]{2,1,0:T(4,128)S(1)} all-gather(s32[1,3,5]{2,1,0:T(4,128)S(1)} %bitcast.80), channel_id=1, replica_groups=mesh['row_0'=4,'row_1'=4,'row_2'=2,'col'=4] {'row_0','row_1','row_2'}, dimensions={0}, use_global_device_ids=true | all-gather | bytes 1980 | tf_op jit(solution)/shard_map/all_gather | solution.py:44
  224.3 5.1 reshape.106
  232.0 14.9 %gather_fusion.1 = bf16[480,96,128]{2,1,0:T(8,128)(2,1)} fusion(bf16[96,96,128]{2,0,1:T(8,128)(2,1)S(1)} %copy.63, s32[1024]{0:T(1024)S(1)} %pad_clamp_fusion), kind=kCustom, calls=%fused_computation.1.clone | custom fusion | bytes 23594880 | tf_op jit(solution)/shard_map/jit(_take)/gather | solution.py:30
  246.8 6.6 %convert_reduce_fusion = f32[96,128]{1,0:T(8,128)S(1)} fusion(bf16[96,5,128,128]{3,2,1,0:T(8,128)(2,1)} %all-gather.7.cloned.1.call-done), kind=kLoop, calls=%fused_computation.4 | loop fusion | flops 15716352 | bytes 15777792 | tf_op jit(solution)/shard_map/reduce_sum | solution.py:46
  253.5 14.1 %convert_reduce_fusion.3 = (f32[]{:T(128)}, f32[96,96,128]{2,0,1:T(8,128)}) fusion(f32[96,128]{1,0:T(8,128)S(1)} %broadcast_divide_fusion, bf16[96,5,128,128]{3,2,1,0:T(8,128)(2,1)} %all-gather.7.cloned.1.call-done, bf16[96,5,96,128]{3,2,1,0:T(8,128)(2,1)} %bitcast.70, pred[96,5]{1,0:T(8,128)(4,1)S(1)} %copy.55), kind=kOutput, calls=%fused_computation.34 | convolution fusion | flops 1520566272 | bytes 32293348 | tf_op jit(solution)/shard_map/cisk,isok->cio/dot_general | solution.py:31
  267.6 7.2 %copy.64 = f32[96,96,128]{2,1,0:T(8,128)} copy(f32[96,96,128]{2,0,1:T(8,128)} %get-tuple-element.18) | data formatting | bytes 9437184 | tf_op jit(solution)/shard_map/cisk,isok->cio/transpose | solution.py:31
  274.8 6.3 reshape.107
  286.1 5.2 all-to-all-start.1
  291.4 6.0 copy.66
  297.5 25.0 %all-reduce.2 = (f32[]{:T(128)}, f32[]{:T(128)}) all-reduce(f32[]{:T(128)} %get-tuple-element.17, f32[]{:T(128)} %get-tuple-element.15), channel_id=1, replica_groups=mesh['row_0'=4,'row_1'=4,'row_2'=2,'col'=4] {'row_0'}, use_global_device_ids=true, to_apply=%region_3.6 | all-reduce | flops 2 | bytes 16 | tf_op jit(solution)/shard_map/psum | solution.py:15
  322.5 11.8 %all-reduce.1 = (f32[]{:T(128)}, f32[]{:T(128)}) all-reduce(f32[]{:T(128)} %get-tuple-element.11, f32[]{:T(128)} %get-tuple-element.12), channel_id=1, replica_groups=mesh['row_0'=4,'row_1'=4,'row_2'=2,'col'=4] {'row_1'}, use_global_device_ids=true, to_apply=%region_4.7 | all-reduce | flops 2 | bytes 16 | tf_op jit(solution)/shard_map/psum | solution.py:15
  337.4 11.1 %all-reduce = (f32[]{:T(128)}, f32[]{:T(128)}) all-reduce(f32[]{:T(128)} %get-tuple-element.13, f32[]{:T(128)} %get-tuple-element.14), channel_id=1, replica_groups=mesh['row_0'=4,'row_1'=4,'row_2'=2,'col'=4] {'col'}, use_global_device_ids=true, to_apply=%region_6.9 | all-reduce | flops 2 | bytes 16 | tf_op jit(solution)/shard_map/psum | solution.py:15
  354.2 86.6 %all-gather.9.cloned.1.call-done = bf16[12288,384]{1,0:T(8,128)(2,1)} async-done(((bf16[3072,384]{1,0:T(8,128)(2,1)}), bf16[12288,384]{1,0:T(8,128)(2,1)}) %all-gather.9.cloned.1.call-update) | async-done | bytes 9437200 | tf_op jit(solution)/shard_map/all_gather | solution.py:52
  440.8 12.3 %gather_fusion.2 = bf16[120,128,384]{2,1,0:T(8,128)(2,1)} fusion(bf16[96,128,384]{2,1,0:T(8,128)(2,1)} %bitcast.73, s32[1024]{0:T(1024)S(1)} %pad_clamp_fusion.1), kind=kCustom, calls=%fused_computation.2.clone | custom fusion | bytes 23593440 | tf_op jit(solution)/shard_map/jit(_take)/gather | solution.py:21
  453.1 8.2 %fusion.5 = f32[24,384,128,1]{1,2,3,0:T(8,128)S(1)} fusion(bf16[24,5,128,128]{3,2,1,0:T(8,128)(2,1)} %param.12, bf16[24,5,128,384]{3,2,1,0:T(8,128)(2,1)} %bitcast.74, pred[24,5]{1,0:T(8,128)(4,1)S(1)} %copy.56), kind=kOutput, calls=%fused_computation.10 | convolution fusion | flops 1515847680 | bytes 20447352 | tf_op jit(solution)/shard_map/jsoi,jsin->jon/dot_general | solution.py:22
  461.9 38.7 %all_to_all.46 = bf16[32,96,384]{2,1,0:T(8,128)(2,1)S(1)} all-to-all(bf16[32,96,384]{2,1,0:T(8,128)(2,1)S(1)} %multiply_convert_fusion.2), channel_id=1, replica_groups=mesh['row_0'=4,'row_1'=4,'row_2'=2,'col'=4] {'row_0','row_1','row_2'}, dimensions={0} | all-to-all | bytes 4718592 | tf_op jit(solution)/shard_map/all_to_all | solution.py:54
  506.5 14.9 %gather_fusion.3 = bf16[480,96,128]{2,1,0:T(8,128)(2,1)} fusion(bf16[96,96,128]{2,0,1:T(8,128)(2,1)S(1)} %copy.70, s32[1024]{0:T(1024)S(1)} %pad_clamp_fusion), kind=kCustom, calls=%fused_computation.3.clone | custom fusion | bytes 23594880 | tf_op jit(solution)/shard_map/jit(_take)/gather | solution.py:30
  521.4 14.1 %convert_reduce_fusion.2 = (f32[]{:T(128)}, f32[96,96,128]{2,0,1:T(8,128)}) fusion(f32[96,128]{1,0:T(8,128)S(1)} %broadcast_divide_fusion, bf16[96,5,128,128]{3,2,1,0:T(8,128)(2,1)} %all-gather.7.cloned.1.call-done, bf16[96,5,96,128]{3,2,1,0:T(8,128)(2,1)} %bitcast.71, pred[96,5]{1,0:T(8,128)(4,1)S(1)} %copy.55), kind=kOutput, calls=%fused_computation.29 | convolution fusion | flops 1520566272 | bytes 32293348 | tf_op jit(solution)/shard_map/cisk,isok->cio/dot_general | solution.py:31
  535.5 7.2 %copy.71 = f32[96,96,128]{2,1,0:T(8,128)} copy(f32[96,96,128]{2,0,1:T(8,128)} %get-tuple-element.20) | data formatting | bytes 9437184 | tf_op jit(solution)/shard_map/cisk,isok->cio/transpose | solution.py:31
  542.7 6.1 reshape.111
  554.0 4.1 all-to-all-start.3
  558.1 31.0 %psum.92 = f32[]{:T(128)} all-reduce(f32[]{:T(128)} %get-tuple-element.19), channel_id=1, replica_groups=mesh['row_0'=4,'row_1'=4,'row_2'=2,'col'=4] {'row_0'}, use_global_device_ids=true, to_apply=%region_13.16 | all-reduce | flops 1 | bytes 8 | tf_op jit(solution)/shard_map/psum | solution.py:15
  589.1 11.7 %psum.93 = f32[]{:T(128)} all-reduce(f32[]{:T(128)} %psum.92), channel_id=1, replica_groups=mesh['row_0'=4,'row_1'=4,'row_2'=2,'col'=4] {'row_1'}, use_global_device_ids=true, to_apply=%region_14.17 | all-reduce | flops 1 | bytes 8 | tf_op jit(solution)/shard_map/psum | solution.py:15
  603.9 10.1 %psum.95 = f32[]{:T(128)} all-reduce(f32[]{:T(128)} %psum.94), channel_id=1, replica_groups=mesh['row_0'=4,'row_1'=4,'row_2'=2,'col'=4] {'col'}, use_global_device_ids=true, to_apply=%region_16.19 | all-reduce | flops 1 | bytes 8 | tf_op jit(solution)/shard_map/psum | solution.py:15
  615.2 5.5 fusion.18
  620.7 6.0 copy.73
  (51 shorter events, 39.1 us)
Async XLA Ops:
  6.5 7.8 %copy-start.1 = (s32[24,5]{0,1:T(8,128)S(1)}, s32[24,5]{0,1:T(8,128)}, u32[]{:S(2)}) copy-start(s32[24,5]{0,1:T(8,128)} %param.13) | copy-start | bytes 1444
  6.5 101.6 %all-gather.5.cloned.1.call-start = ((), (), s32[]{:S(2)}) async-start(), calls=%async_computation.4 | async-start | bytes 11796480 | tf_op jit(solution)/shard_map/all_gather | solution.py:52
  13.5 233.3 %all-gather.7.cloned.1.call-start = ((), (), s32[]{:S(2)}) async-start(), calls=%async_computation.5 | async-start | bytes 16220160 | tf_op jit(solution)/shard_map/all_gather | solution.py:43
  141.7 9.1 %copy-start.2 = (s32[3,5]{1,0:T(4,128)S(1)}, s32[3,5]{1,0:T(4,128)}, u32[]{:S(2)}) copy-start(s32[3,5]{1,0:T(4,128)} %param.11) | copy-start | bytes 184
  143.6 78.4 %all-to-all-start = ((bf16[32,96,384]{2,1,0:T(8,128)(2,1)}), bf16[32,96,384]{2,1,0:T(8,128)(2,1)S(1)}, u32[]{:S(2)}, u32[]{:S(2)}) async-start(bf16[32,96,384]{2,1,0:T(8,128)(2,1)} %multiply_convert_fusion.5), calls=%async_computation | async-start | bytes 4718592 | tf_op jit(solution)/shard_map/all_to_all | solution.py:54
  286.1 63.6 %all-to-all-start.1 = ((bf16[96,32,384]{2,0,1:T(8,128)(2,1)}), bf16[96,32,384]{2,0,1:T(8,128)(2,1)S(1)}, u32[]{:S(2)}, u32[]{:S(2)}) async-start(bf16[96,32,384]{2,0,1:T(8,128)(2,1)} %copy.65), calls=%async_computation.1 | async-start | bytes 4718592 | tf_op jit(solution)/shard_map/all_to_all | solution.py:57
  291.4 149.4 %all-gather.9.cloned.1.call-start = ((), (), s32[]{:S(2)}) async-start(), calls=%async_computation.6 | async-start | bytes 11796480 | tf_op jit(solution)/shard_map/all_gather | solution.py:52
  349.8 2.3 copy-start
  554.0 60.5 %all-to-all-start.3 = ((bf16[96,32,384]{2,0,1:T(8,128)(2,1)}), bf16[96,32,384]{2,0,1:T(8,128)(2,1)S(1)}, u32[]{:S(2)}, u32[]{:S(2)}) async-start(bf16[96,32,384]{2,0,1:T(8,128)(2,1)} %copy.72), calls=%async_computation.3 | async-start | bytes 4718592 | tf_op jit(solution)/shard_map/all_to_all | solution.py:57
Sparse Core Ops, SparseCore 0:
  13.7 94.4 all-gather.4
  110.4 95.9 all-gather.6
  354.3 86.4 all-gather.8
where the time goes:
time: 642 us; the launch traced here: 633 us
  blocking collectives  216 us (34%)
  waiting for transfers between devices  178 us (28%)
  local copies, waits for them, and re-layouts  129 us (20%)
  matrix products  44.8 us (7%)
  other arithmetic  33.4 us (5%)
  starting transfers between devices  16.6 us (3%)
  between operations  15.3 us (2%)
    all_gather x2, waiting for transfers between devices, local(): gathered = lax.all_gather(current, 'col', axis=0, tiled=True)  177 us
    psum x8, blocking collectives, by_axis(): return functools.reduce(lax.psum, axes, value)  107 us
    all_gather x1, blocking collectives, local(): lax.all_gather(columns_first, ROW, axis=0, tiled=True)  70.6 us
    all_to_all x1, blocking collectives, local(): lax.all_to_all(mixed_cols, ROW, split_axis=0, concat_axis=1, tiled=True)  38.7 us
    gather x2, local copies, waits for them, and re-layouts, first_product(): picked = jnp.take(blocks, columns, axis=1)  29.8 us
    dot_general x2, matrix products, first_product(): jnp.einsum('cisk,isok->cio', picked, tile_set, preferred_element_type=jnp...  28.2 us
    gather x2, local copies, waits for them, and re-layouts, second_product(): picked = jnp.take(blocks, columns, axis=0)  25 us
    dot_general x2, matrix products, second_product(): jnp.einsum('jsoi,jsin->jon', tile_set, picked, preferred_element_type=jnp...  16.5 us
  transfers between devices with their start and end apart: 6, of which 2 were waited for; matrix products, arithmetic and copies ran while one was open for 11% of the time, Pallas kernels for 0%

commit v1 on v0

--- a/solution.py
+++ b/solution.py
@@ -51,7 +51,10 @@
         current = current_state.astype(jnp.bfloat16)
         gathered = lax.all_gather(current, "col", axis=0, tiled=True)
         mixed_cols = second_product(gathered, tiles_second, columns_second, inverse_second)
-        slab_data = lax.all_to_all(mixed_cols, ROW, split_axis=0, concat_axis=1, tiled=True)
+        n_dev = lax.axis_size(ROW)
+        pieces = jnp.stack(jnp.split(mixed_cols, n_dev, axis=0), axis=0)
+        pieces = lax.all_to_all(pieces, ROW, split_axis=0, concat_axis=0)
+        slab_data = jnp.concatenate(pieces, axis=1)
         propagated = first_product(slab_data, all_first, all_columns, inverse_first)
         partial_value = jnp.sum(propagated.astype(jnp.float32))
         returned = lax.all_to_all(propagated, ROW, split_axis=1, concat_axis=0, tiled=True)

time: 642 us -> 643 us (level)
  local copies, waits for them, and re-layouts: 129 us -> 150 us
  blocking collectives: 216 us -> 197 us
    unnamed x9 -> x71, local copies, waits for them, and re-layouts: 7.85 us -> 28.2 us
    all_gather x1, blocking collectives: 70.6 us -> 51.6 us  [local(): lax.all_gather(columns_first, ROW, axis=0, tiled=True)]
    another operation x0 -> x6, local copies, waits for them, and re-layouts: none -> 13.4 us  [the longest x4 12.8 us: first_product(): blocks = slab_data.reshape(slab_data.shape[0], -1, tile_size)]
    reshape x4 -> x2, local copies, waits for them, and re-layouts: 12.8 us -> 3.1 us  [local(): slab_data = jnp.concatenate(pieces, axis=1)]
  transfers between devices with their start and end apart: 6 -> 6, of which waited for: 2 -> 2; matrix products, arithmetic and copies ran while one was open for 11% -> 14% of each run, Pallas kernels for 0% -> 0%
where the time goes in v1:
time: 643 us; the launch traced here: 634 us
  blocking collectives  197 us (31%)
  waiting for transfers between devices  178 us (28%)
  local copies, waits for them, and re-layouts  150 us (23%)
  matrix products  44.8 us (7%)
  other arithmetic  32 us (5%)
  starting transfers between devices  16.8 us (3%)
  between operations  15.5 us (2%)
    all_gather x2, waiting for transfers between devices, local(): gathered = lax.all_gather(current, 'col', axis=0, tiled=True)  177 us
    psum x8, blocking collectives, by_axis(): return functools.reduce(lax.psum, axes, value)  107 us
    all_gather x1, blocking collectives, local(): lax.all_gather(columns_first, ROW, axis=0, tiled=True)  51.6 us
    all_to_all x1, blocking collectives, local(): pieces = lax.all_to_all(pieces, ROW, split_axis=0, concat_axis=0)  38.7 us
    gather x2, local copies, waits for them, and re-layouts, first_product(): picked = jnp.take(blocks, columns, axis=1)  29.8 us
    dot_general x2, matrix products, first_product(): jnp.einsum('cisk,isok->cio', picked, tile_set, preferred_element_type=jnp...  28.2 us
    unnamed x71, local copies, waits for them, and re-layouts  28.2 us
    gather x2, local copies, waits for them, and re-layouts, second_product(): picked = jnp.take(blocks, columns, axis=0)  25 us
  transfers between devices with their start and end apart: 6, of which 2 were waited for; matrix products, arithmetic and copies ran while one was open for 14% of the time, Pallas kernels for 0%

profile of v1, /device:TPU:0, one launch (start us, length us, event | category | flops | bytes accessed | tf_op | source)
XLA Modules:
  0.0 634.5 jit_solution(3374534732944684079)
XLA Ops:
  6.5 7.0 %fusion.33 = (f32[]{:T(128)}, bf16[3072,384]{0,1:T(8,128)(2,1)}) fusion(f32[384,3072]{1,0:T(8,128)} %param.9), kind=kLoop, calls=%fused_computation.184 | loop fusion | flops 2359295 | bytes 7077892 | tf_op jit(solution)/shard_map/reduce_sum | solution.py:48
  17.3 90.8 %all-gather.5.cloned.1.call-done = bf16[12288,384]{0,1:T(8,128)(2,1)} async-done(((bf16[3072,384]{0,1:T(8,128)(2,1)}), bf16[12288,384]{0,1:T(8,128)(2,1)}) %all-gather.5.cloned.1.call-update) | async-done | bytes 9437200 | tf_op jit(solution)/shard_map/all_gather | solution.py:52
  108.1 12.6 %copy.88 = bf16[12288,384]{1,0:T(8,128)(2,1)} copy(bf16[12288,384]{0,1:T(8,128)(2,1)} %all-gather.5.cloned.1.call-done) | data formatting | bytes 18874368 | tf_op jit(solution)/shard_map/all_gather | solution.py:52
  120.7 12.7 %gather_fusion = bf16[120,128,384]{2,1,0:T(8,128)(2,1)} fusion(bf16[96,128,384]{2,1,0:T(8,128)(2,1)} %bitcast.333, s32[1024]{0:T(1024)S(1)} %pad_clamp_fusion.1), kind=kCustom, calls=%fused_computation.clone | custom fusion | bytes 23593440 | tf_op jit(solution)/shard_map/jit(_take)/gather | solution.py:21
  133.4 8.3 %fusion.8 = f32[24,384,128,1]{1,2,3,0:T(8,128)S(1)} fusion(bf16[24,5,128,128]{3,2,1,0:T(8,128)(2,1)} %param.12, bf16[24,5,128,384]{3,2,1,0:T(8,128)(2,1)} %bitcast.339, pred[24,5]{1,0:T(8,128)(4,1)S(1)} %copy.85), kind=kOutput, calls=%fused_computation.13 | convolution fusion | flops 1515847680 | bytes 20447352 | tf_op jit(solution)/shard_map/jsoi,jsin->jon/dot_general | solution.py:22
  162.7 7.4 %all-to-all-start = ((bf16[32,96,384]{2,1,0:T(8,128)(2,1)}), bf16[32,96,384]{2,1,0:T(8,128)(2,1)S(1)}, u32[]{:S(2)}, u32[]{:S(2)}) async-start(bf16[32,96,384]{2,1,0:T(8,128)(2,1)} %constant_dynamic-update-slice_fusion), calls=%async_computation | async-start | bytes 4718592 | tf_op jit(solution)/shard_map/all_to_all | solution.py:56
  170.1 51.6 %all-gather = s32[32,3,5]{2,1,0:T(4,128)S(1)} all-gather(s32[1,3,5]{2,1,0:T(4,128)S(1)} %bitcast.342), channel_id=1, replica_groups=mesh['row_0'=4,'row_1'=4,'row_2'=2,'col'=4] {'row_0','row_1','row_2'}, dimensions={0}, use_global_device_ids=true | all-gather | bytes 1980 | tf_op jit(solution)/shard_map/all_gather | solution.py:44
  224.5 5.1 reshape_reshape.6
  232.2 14.9 %gather_fusion.1 = bf16[480,96,128]{2,1,0:T(8,128)(2,1)} fusion(bf16[96,96,128]{2,0,1:T(8,128)(2,1)S(1)} %copy.92, s32[1024]{0:T(1024)S(1)} %pad_clamp_fusion), kind=kCustom, calls=%fused_computation.1.clone | custom fusion | bytes 23594880 | tf_op jit(solution)/shard_map/jit(_take)/gather | solution.py:30
  247.1 6.6 %convert_reduce_fusion = f32[96,128]{1,0:T(8,128)S(1)} fusion(bf16[96,5,128,128]{3,2,1,0:T(8,128)(2,1)} %all-gather.7.cloned.1.call-done), kind=kLoop, calls=%fused_computation.4 | loop fusion | flops 15716352 | bytes 15777792 | tf_op jit(solution)/shard_map/reduce_sum | solution.py:46
  253.8 14.1 %convert_reduce_fusion.3 = (f32[]{:T(128)}, f32[96,96,128]{2,0,1:T(8,128)}) fusion(f32[96,128]{1,0:T(8,128)S(1)} %broadcast_divide_fusion, bf16[96,5,128,128]{3,2,1,0:T(8,128)(2,1)} %all-gather.7.cloned.1.call-done, bf16[96,5,96,128]{3,2,1,0:T(8,128)(2,1)} %bitcast.334, pred[96,5]{1,0:T(8,128)(4,1)S(1)} %copy.84), kind=kOutput, calls=%fused_computation.37 | convolution fusion | flops 1520566272 | bytes 32293348 | tf_op jit(solution)/shard_map/cisk,isok->cio/dot_general | solution.py:31
  267.8 7.2 %copy.93 = f32[96,96,128]{2,1,0:T(8,128)} copy(f32[96,96,128]{2,0,1:T(8,128)} %get-tuple-element.18) | data formatting | bytes 9437184 | tf_op jit(solution)/shard_map/cisk,isok->cio/transpose | solution.py:31
  275.0 6.3 reshape.87
  286.4 5.3 all-to-all-start.1
  291.8 6.0 copy.95
  297.8 25.0 %all-reduce.2 = (f32[]{:T(128)}, f32[]{:T(128)}) all-reduce(f32[]{:T(128)} %get-tuple-element.17, f32[]{:T(128)} %get-tuple-element.15), channel_id=1, replica_groups=mesh['row_0'=4,'row_1'=4,'row_2'=2,'col'=4] {'row_0'}, use_global_device_ids=true, to_apply=%region_3.6 | all-reduce | flops 2 | bytes 16 | tf_op jit(solution)/shard_map/psum | solution.py:15
  322.8 11.8 %all-reduce.1 = (f32[]{:T(128)}, f32[]{:T(128)}) all-reduce(f32[]{:T(128)} %get-tuple-element.11, f32[]{:T(128)} %get-tuple-element.12), channel_id=1, replica_groups=mesh['row_0'=4,'row_1'=4,'row_2'=2,'col'=4] {'row_1'}, use_global_device_ids=true, to_apply=%region_4.7 | all-reduce | flops 2 | bytes 16 | tf_op jit(solution)/shard_map/psum | solution.py:15
  337.7 11.1 %all-reduce = (f32[]{:T(128)}, f32[]{:T(128)}) all-reduce(f32[]{:T(128)} %get-tuple-element.13, f32[]{:T(128)} %get-tuple-element.14), channel_id=1, replica_groups=mesh['row_0'=4,'row_1'=4,'row_2'=2,'col'=4] {'col'}, use_global_device_ids=true, to_apply=%region_6.9 | all-reduce | flops 2 | bytes 16 | tf_op jit(solution)/shard_map/psum | solution.py:15
  354.5 86.6 %all-gather.9.cloned.1.call-done = bf16[12288,384]{1,0:T(8,128)(2,1)} async-done(((bf16[3072,384]{1,0:T(8,128)(2,1)}), bf16[12288,384]{1,0:T(8,128)(2,1)}) %all-gather.9.cloned.1.call-update) | async-done | bytes 9437200 | tf_op jit(solution)/shard_map/all_gather | solution.py:52
  441.1 12.3 %gather_fusion.2 = bf16[120,128,384]{2,1,0:T(8,128)(2,1)} fusion(bf16[96,128,384]{2,1,0:T(8,128)(2,1)} %bitcast.337, s32[1024]{0:T(1024)S(1)} %pad_clamp_fusion.1), kind=kCustom, calls=%fused_computation.2.clone | custom fusion | bytes 23593440 | tf_op jit(solution)/shard_map/jit(_take)/gather | solution.py:21
  453.5 8.2 %fusion.5 = f32[24,384,128,1]{1,2,3,0:T(8,128)S(1)} fusion(bf16[24,5,128,128]{3,2,1,0:T(8,128)(2,1)} %param.12, bf16[24,5,128,384]{3,2,1,0:T(8,128)(2,1)} %bitcast.338, pred[24,5]{1,0:T(8,128)(4,1)S(1)} %copy.85), kind=kOutput, calls=%fused_computation.10 | convolution fusion | flops 1515847680 | bytes 20447352 | tf_op jit(solution)/shard_map/jsoi,jsin->jon/dot_general | solution.py:22
  462.9 38.7 %all_to_all.30 = bf16[32,96,384]{2,1,0:T(8,128)(2,1)S(1)} all-to-all(bf16[32,96,384]{2,1,0:T(8,128)(2,1)S(1)} %constant_dynamic-update-slice_fusion.32), channel_id=1, replica_groups=mesh['row_0'=4,'row_1'=4,'row_2'=2,'col'=4] {'row_0','row_1','row_2'}, dimensions={0} | all-to-all | bytes 4718592 | tf_op jit(solution)/shard_map/all_to_all | solution.py:56
  507.5 14.9 %gather_fusion.3 = bf16[480,96,128]{2,1,0:T(8,128)(2,1)} fusion(bf16[96,96,128]{2,0,1:T(8,128)(2,1)S(1)} %copy.99, s32[1024]{0:T(1024)S(1)} %pad_clamp_fusion), kind=kCustom, calls=%fused_computation.3.clone | custom fusion | bytes 23594880 | tf_op jit(solution)/shard_map/jit(_take)/gather | solution.py:30
  522.4 14.1 %convert_reduce_fusion.2 = (f32[]{:T(128)}, f32[96,96,128]{2,0,1:T(8,128)}) fusion(f32[96,128]{1,0:T(8,128)S(1)} %broadcast_divide_fusion, bf16[96,5,128,128]{3,2,1,0:T(8,128)(2,1)} %all-gather.7.cloned.1.call-done, bf16[96,5,96,128]{3,2,1,0:T(8,128)(2,1)} %bitcast.335, pred[96,5]{1,0:T(8,128)(4,1)S(1)} %copy.84), kind=kOutput, calls=%fused_computation.33 | convolution fusion | flops 1520566272 | bytes 32293348 | tf_op jit(solution)/shard_map/cisk,isok->cio/dot_general | solution.py:31
  536.6 7.2 %copy.100 = f32[96,96,128]{2,1,0:T(8,128)} copy(f32[96,96,128]{2,0,1:T(8,128)} %get-tuple-element.20) | data formatting | bytes 9437184 | tf_op jit(solution)/shard_map/cisk,isok->cio/transpose | solution.py:31
  543.7 6.1 reshape.91
  555.0 4.1 all-to-all-start.3
  559.1 31.0 %psum.92 = f32[]{:T(128)} all-reduce(f32[]{:T(128)} %get-tuple-element.19), channel_id=1, replica_groups=mesh['row_0'=4,'row_1'=4,'row_2'=2,'col'=4] {'row_0'}, use_global_device_ids=true, to_apply=%region_13.16 | all-reduce | flops 1 | bytes 8 | tf_op jit(solution)/shard_map/psum | solution.py:15
  590.1 11.7 %psum.93 = f32[]{:T(128)} all-reduce(f32[]{:T(128)} %psum.92), channel_id=1, replica_groups=mesh['row_0'=4,'row_1'=4,'row_2'=2,'col'=4] {'row_1'}, use_global_device_ids=true, to_apply=%region_14.17 | all-reduce | flops 1 | bytes 8 | tf_op jit(solution)/shard_map/psum | solution.py:15
  604.9 10.1 %psum.95 = f32[]{:T(128)} all-reduce(f32[]{:T(128)} %psum.94), channel_id=1, replica_groups=mesh['row_0'=4,'row_1'=4,'row_2'=2,'col'=4] {'col'}, use_global_device_ids=true, to_apply=%region_16.19 | all-reduce | flops 1 | bytes 8 | tf_op jit(solution)/shard_map/psum | solution.py:15
  616.2 5.5 fusion.18
  621.7 6.0 copy.102
  (114 shorter events, 58.6 us)
Async XLA Ops:
  6.5 101.6 %all-gather.5.cloned.1.call-start = ((), (), s32[]{:S(2)}) async-start(), calls=%async_computation.4 | async-start | bytes 11796480 | tf_op jit(solution)/shard_map/all_gather | solution.py:52
  13.5 0.8 copy-start.1
  13.5 233.6 %all-gather.7.cloned.1.call-start = ((), (), s32[]{:S(2)}) async-start(), calls=%async_computation.5 | async-start | bytes 16220160 | tf_op jit(solution)/shard_map/all_gather | solution.py:43
  162.7 7.4 %copy-start.2 = (s32[3,5]{1,0:T(4,128)S(1)}, s32[3,5]{1,0:T(4,128)}, u32[]{:S(2)}) copy-start(s32[3,5]{1,0:T(4,128)} %param.11) | copy-start | bytes 184
  162.7 59.6 %all-to-all-start = ((bf16[32,96,384]{2,1,0:T(8,128)(2,1)}), bf16[32,96,384]{2,1,0:T(8,128)(2,1)S(1)}, u32[]{:S(2)}, u32[]{:S(2)}) async-start(bf16[32,96,384]{2,1,0:T(8,128)(2,1)} %constant_dynamic-update-slice_fusion), calls=%async_computation | async-start | bytes 4718592 | tf_op jit(solution)/shard_map/all_to_all | solution.py:56
  286.4 63.7 %all-to-all-start.1 = ((bf16[96,32,384]{2,0,1:T(8,128)(2,1)}), bf16[96,32,384]{2,0,1:T(8,128)(2,1)S(1)}, u32[]{:S(2)}, u32[]{:S(2)}) async-start(bf16[96,32,384]{2,0,1:T(8,128)(2,1)} %copy.94), calls=%async_computation.1 | async-start | bytes 4718592 | tf_op jit(solution)/shard_map/all_to_all | solution.py:60
  291.7 149.4 %all-gather.9.cloned.1.call-start = ((), (), s32[]{:S(2)}) async-start(), calls=%async_computation.6 | async-start | bytes 11796480 | tf_op jit(solution)/shard_map/all_gather | solution.py:52
  350.1 2.3 copy-start
  555.0 60.5 %all-to-all-start.3 = ((bf16[96,32,384]{2,0,1:T(8,128)(2,1)}), bf16[96,32,384]{2,0,1:T(8,128)(2,1)S(1)}, u32[]{:S(2)}, u32[]{:S(2)}) async-start(bf16[96,32,384]{2,0,1:T(8,128)(2,1)} %copy.101), calls=%async_computation.3 | async-start | bytes 4718592 | tf_op jit(solution)/shard_map/all_to_all | solution.py:60
Sparse Core Ops, SparseCore 0:
  13.7 94.4 all-gather.4
  110.4 88.8 all-gather.6
  354.7 86.4 all-gather.8
